TPU v7x, 256 devices: a 2x2x32 block of a 4x8x32 slice. The times are simulated.
256 devices in a mesh: groups: 4 (over x, y), blk: 64 (over z, core).
Axes of the slice: x: 2, y: 2, z: 32, core: 2. Of those that a mesh axis runs over, the one named last changes fastest.
The devices are a block of a 4x8x32 slice.
Arguments:
- queries: bfloat16 [128, 64, 2048], P('blk', 'groups'), parts along dimension 1, may hold values from -24 to 24
- keys: bfloat16 [524288, 512], P(('groups', 'blk')), parts along dimension 0, may hold values from -24 to 24
- values: bfloat16 [524288, 512], P(('groups', 'blk')), parts along dimension 0, may hold values from -24 to 24
- out_weight: bfloat16 [2048, 2048], replicated, may hold values from -0.125 to 0.125
- chosen: int32 [64, 12], P('groups'), parts along dimension 0, may hold values from 0 to 255, as said below
- tile_start: int32 [64], P('groups'), parts along dimension 0, may hold values from 0 to 130944, as said below
Outputs:
- projected: bfloat16 [128, 64, 2048], P('blk', 'groups'), parts along dimension 1
There are 4 independent parts, one for each index of `groups`. A program takes and returns all parts, laid end to end along the dimension named above; an argument that names none is the same for every part. Nothing has to cross between parts.
Inputs may be any that keep to these rules, and one draw needn't show every extreme that they name: `chosen`: row t lists 12 different blocks; the first is the block that holds tile t's positions, the others lie before it. Each block is listed by at most 2 tiles, and some block by exactly 2. `tile_start[t]` is a multiple of 128; tile t's queries have positions tile_start[t] to tile_start[t] + 127, all inside block chosen[t, 0].
All inputs are finite; a program needn't handle non-finite values.
Results may differ from a plain program's by a relative error of at most 0.0064.
Values may be sent and summed in bfloat16 or wider, within the bound.
A program may use at most 128 MiB of HBM per device.

v0:
```python
import math
import jax
import jax.numpy as jnp
from jax import lax
from jax.sharding import PartitionSpec as P

QH = 16
KVH = 4
HD = 128
BLOCK = 512
CAP = 2
neg_big = -1e30


def visit_block(query_tile, tile_begin, block_keys, block_values, block_begin):
    tile_rows = query_tile.shape[0]
    key_count = block_keys.shape[0]
    query_view = query_tile.reshape(tile_rows, KVH, QH // KVH, HD)
    key_view = block_keys.reshape(key_count, KVH, HD)
    value_view = block_values.reshape(key_count, KVH, HD)
    scores = jnp.einsum(
        "rkgd,jkd->kgrj", query_view, key_view, preferred_element_type=jnp.float32
    ) * (1.0 / math.sqrt(HD))
    query_pos = tile_begin + jnp.arange(tile_rows, dtype=jnp.int32)
    key_pos = block_begin + jnp.arange(key_count, dtype=jnp.int32)
    visible = key_pos[None, :] <= query_pos[:, None]
    masked = jnp.where(visible, scores, neg_big)
    highest = jnp.max(masked, axis=3, keepdims=True)
    summed = jnp.sum(jnp.where(visible, jnp.exp(masked - highest), 0.0), axis=3, keepdims=True)
    log_total = highest + jnp.log(summed)
    weights = jnp.where(visible, jnp.exp(masked - log_total), 0.0).astype(jnp.bfloat16)
    partial_value = jnp.einsum(
        "kgrj,jkd->rkgd", weights, value_view, preferred_element_type=jnp.float32
    )
    partial_value = partial_value.astype(jnp.bfloat16).reshape(tile_rows, QH * HD)
    log_rows = jnp.transpose(log_total[..., 0], (2, 0, 1)).reshape(tile_rows, QH)
    return (partial_value, log_rows)


def slot_table(chosen, block_count):
    tile_count = chosen.shape[0]
    block_ids = jnp.arange(block_count, dtype=jnp.int32)
    tile_index = jnp.arange(tile_count, dtype=jnp.int32)
    member = jnp.any(chosen[None, :, :] == block_ids[:, None, None], axis=2)
    ranking = jnp.cumsum(member.astype(jnp.int32), axis=1) - 1
    slot_index = jnp.arange(CAP, dtype=jnp.int32)
    hits = member[:, None, :] & (ranking[:, None, :] == slot_index[None, :, None])
    slot_tile = jnp.sum(jnp.where(hits, tile_index[None, None, :], 0), axis=2)
    slot_live = jnp.any(hits, axis=2)
    return (hits, slot_tile, slot_live)


def on_device(queries, keys, values, out_weight, chosen, tile_start):
    owner_count = lax.axis_size("blk")
    owner_dev = lax.axis_index("blk")
    local_rows, tile_count, width = queries.shape
    per_device = keys.shape[0] // BLOCK
    slot_count = per_device * CAP
    head_count = QH
    hits_blocks, tiles_blocks, live_blocks = slot_table(chosen, owner_count * per_device)
    tiles_all = tiles_blocks.reshape(owner_count, slot_count)
    live_all = live_blocks.reshape(owner_count, slot_count)
    my_tiles = tiles_all[owner_dev]
    my_live = live_all[owner_dev]
    begins = tile_start[my_tiles]
    local_block = jnp.arange(slot_count, dtype=jnp.int32) // CAP
    gathered = lax.all_gather(queries, "blk", axis=0, tiled=True)
    slot_queries = jnp.transpose(jnp.take(gathered, my_tiles, axis=1), (1, 0, 2))

    def one_slot(inputs):
        query_tile, tile_begin, block_here = inputs
        offset = block_here * BLOCK
        block_keys = lax.dynamic_slice_in_dim(keys, offset, BLOCK, 0)
        block_values = lax.dynamic_slice_in_dim(values, offset, BLOCK, 0)
        block_begin = (owner_dev * per_device + block_here) * BLOCK
        return visit_block(query_tile, tile_begin, block_keys, block_values, block_begin)

    partials, log_slots = lax.map(one_slot, (slot_queries, begins, local_block))
    log_slots = jnp.where(my_live[:, None, None], log_slots, neg_big)
    part_out = partials.reshape(slot_count, owner_count, local_rows, width)
    peak_out = log_slots.reshape(slot_count, owner_count, local_rows, head_count)
    got_parts = lax.all_to_all(part_out, "blk", split_axis=1, concat_axis=1, tiled=True)
    got_peaks = lax.all_to_all(peak_out, "blk", split_axis=1, concat_axis=1, tiled=True)
    pair_count = slot_count * owner_count
    pair_tile = jnp.transpose(tiles_all).reshape(pair_count)
    pair_live = jnp.transpose(live_all).reshape(pair_count)
    tile_index = jnp.arange(tile_count, dtype=jnp.int32)
    pair_hits = (pair_tile[None, :] == tile_index[:, None]) & pair_live[None, :]
    peaks = got_peaks.reshape(pair_count, local_rows, head_count)
    tile_peak = jnp.max(jnp.where(pair_hits[:, :, None, None], peaks[None], neg_big), axis=1)
    pair_peak = tile_peak[pair_tile]
    factor = jnp.where(pair_live[:, None, None], jnp.exp(peaks - pair_peak), 0.0)
    weighted = factor[..., None] * got_parts.reshape(pair_count, local_rows, head_count, -1).astype(
        jnp.float32
    )
    weighted = weighted.reshape(pair_count, local_rows, width)
    pick_table = pair_hits.astype(jnp.float32)
    numer_rows = jnp.einsum("tp,prf->rtf", pick_table, weighted, precision=lax.Precision.HIGHEST)
    denom_rows = jnp.einsum("tp,prh->rth", pick_table, factor, precision=lax.Precision.HIGHEST)
    merged = numer_rows.reshape(local_rows, tile_count, head_count, -1) / denom_rows[..., None]
    merged = merged.reshape(local_rows * tile_count, width).astype(jnp.bfloat16)
    result = jnp.dot(merged, out_weight, preferred_element_type=jnp.float32).astype(jnp.bfloat16)
    return result.reshape(local_rows, tile_count, out_weight.shape[1])


def solution(mesh):
    placed = (
        P("blk", "groups", None),
        P(("groups", "blk"), None),
        P(("groups", "blk"), None),
        P(),
        P("groups", None),
        P("groups"),
    )
    return jax.shard_map(
        on_device, mesh=mesh, in_specs=placed, out_specs=P("blk", "groups", None), check_vma=False
    )
```

profile of v0, /device:TPU:38, one launch (start us, length us, event | category | flops | bytes accessed | tf_op | source)
XLA Modules:
  0.0 728.5 jit_solution(17762847718979088911)
XLA Ops:
  9.6 149.9 %all-gather.2.cloned.1.call-done = bf16[128,16,2048]{2,1,0:T(8,128)(2,1)} async-done(((bf16[2,16,2048]{2,1,0:T(8,128)(2,1)}), bf16[128,16,2048]{2,1,0:T(8,128)(2,1)}) %all-gather.2.cloned.1.call-update) | async-done | bytes 8388624 | tf_op jit(solution)/shard_map/all_gather | solution.py:67
  159.5 11.2 %copy.79 = bf16[128,16,2048]{2,0,1:T(8,128)(2,1)} copy(bf16[128,16,2048]{2,1,0:T(8,128)(2,1)} %all-gather.2.cloned.1.call-done) | data formatting | bytes 16777216 | tf_op jit(solution)/shard_map/all_gather | solution.py:67
  170.7 6.1 gather_fusion.1
  176.9 4.6 broadcast_select_fusion
  181.4 81.9 %while.14 = (s32[]{:T(128)}, bf16[8,128,2048]{1,2,0:T(8,128)(2,1)}, f32[8,128,16]{1,2,0:T(8,128)S(1)}, s32[8]{0:T(128)S(1)}, bf16[2048,512]{1,0:T(8,128)(2,1)}, ...) while((s32[]{:T(128)}, bf16[8,128,2048]{1,2,0:T(8,128)(2,1)}, ...), condition=%wide.region_7.8_spmd, body=%wide.region_4.7_spmd.sunk | while | flops 550828672 | bytes 22361340 | solution.py:78
  182.7 1.3 constant_dynamic-slice_fusion.6
  192.9 1.3 constant_dynamic-slice_fusion.6
  203.1 1.3 constant_dynamic-slice_fusion.6
  213.4 1.3 constant_dynamic-slice_fusion.6
  223.6 1.3 constant_dynamic-slice_fusion.6
  244.1 1.3 constant_dynamic-slice_fusion.6
  264.5 14.5 %all-to-all-start = ((f32[64,1,256]{2,1,0:T(1,128)}), f32[64,1,256]{2,1,0:T(1,128)S(1)}, u32[]{:S(2)}, u32[]{:S(2)}) async-start(f32[64,1,256]{2,1,0:T(1,128)} %reshape.230), calls=%async_computation | async-start | bytes 131072 | tf_op jit(solution)/shard_map/all_to_all | solution.py:83
  279.0 6.7 copy.89
  285.7 18.1 %all-to-all-done = f32[64,1,256]{2,1,0:T(1,128)S(1)} async-done(((f32[64,1,256]{2,1,0:T(1,128)}), f32[64,1,256]{2,1,0:T(1,128)S(1)}, u32[]{:S(2)}, u32[]{:S(2)}) %all-to-all-start) | async-done | bytes 65568 | tf_op jit(solution)/shard_map/all_to_all | solution.py:83
  303.9 7.3 %all-to-all-start.1 = ((bf16[8,64,2,2048]{3,0,2,1:T(8,128)(2,1)}), bf16[8,64,2,2048]{3,0,2,1:T(8,128)(2,1)}, u32[]{:S(2)}, u32[]{:S(2)}) async-start(bf16[8,64,2,2048]{3,0,2,1:T(8,128)(2,1)} %bitcast.114), calls=%async_computation.1 | async-start | bytes 8388608 | tf_op jit(solution)/shard_map/all_to_all | solution.py:82
  313.8 2.1 gather_fusion.2
  315.9 1.8 exponential_select_fusion
  318.3 5.1 mul.35
  323.4 9.3 %mul.36 = f32[512,2,2048]{2,0,1:T(8,128)} reshape(f32[512,2,16,128]{3,2,0,1:T(8,128)} %mul.35) | data formatting | bytes 16777216 | tf_op jit(solution)/shard_map/mul | solution.py:93
  332.7 357.4 %all-to-all-done.1 = bf16[8,64,2,2048]{3,0,2,1:T(8,128)(2,1)} async-done(((bf16[8,64,2,2048]{3,0,2,1:T(8,128)(2,1)}), bf16[8,64,2,2048]{3,0,2,1:T(8,128)(2,1)}, u32[]{:S(2)}, u32[]{:S(2)}) %all-to-all-start.1) | async-done | bytes 4194336 | tf_op jit(solution)/shard_map/all_to_all | solution.py:82
  690.1 7.8 %copy.90 = f32[8,64,2,2048]{3,1,0,2:T(8,128)} copy(bf16[8,64,2,2048]{3,0,2,1:T(8,128)(2,1)} %all-to-all-done.1) | data formatting | bytes 12582912 | tf_op jit(solution)/shard_map/convert_element_type | solution.py:93
  697.9 11.7 %bitcast_multiply_fusion = f32[512,2,2048]{2,0,1:T(8,128)} fusion(f32[512,2,2048]{2,0,1:T(8,128)} %mul.36, f32[8,64,2,2048]{3,1,0,2:T(8,128)} %copy.90), kind=kLoop, calls=%fused_computation.22 | loop fusion | flops 2097152 | bytes 25165824 | tf_op jit(solution)/shard_map/mul | solution.py:93
  709.6 6.1 fusion.13
  716.0 5.6 convolution_convert_fusion
  (169 shorter events, 71.4 us)
Async XLA Ops:
  6.5 2.4 copy-start
  6.6 153.0 %all-gather.2.cloned.1.call-start = ((), (), s32[]{:S(2)}) async-start(), calls=%async_computation.2 | async-start | bytes 8519680 | tf_op jit(solution)/shard_map/all_gather | solution.py:67
  264.5 39.4 %all-to-all-start = ((f32[64,1,256]{2,1,0:T(1,128)}), f32[64,1,256]{2,1,0:T(1,128)S(1)}, u32[]{:S(2)}, u32[]{:S(2)}) async-start(f32[64,1,256]{2,1,0:T(1,128)} %reshape.230), calls=%async_computation | async-start | bytes 131072 | tf_op jit(solution)/shard_map/all_to_all | solution.py:83
  303.9 386.3 %all-to-all-start.1 = ((bf16[8,64,2,2048]{3,0,2,1:T(8,128)(2,1)}), bf16[8,64,2,2048]{3,0,2,1:T(8,128)(2,1)}, u32[]{:S(2)}, u32[]{:S(2)}) async-start(bf16[8,64,2,2048]{3,0,2,1:T(8,128)(2,1)} %bitcast.114), calls=%async_computation.1 | async-start | bytes 8388608 | tf_op jit(solution)/shard_map/all_to_all | solution.py:82
  715.9 5.7 copy-start.1
Sparse Core Ops, SparseCore 0:
  9.2 150.2 all-gather.1
where the time goes:
time: 730 us; the launch traced here: 728 us
  waiting for transfers between devices  526 us (72%)
  local copies, waits for them, and re-layouts  94.1 us (13%)
  other arithmetic  33.9 us (5%)
  matrix products  28.4 us (4%)
  starting transfers between devices  21.8 us (3%)
  between operations  13.6 us (2%)
  loops' own time  10.4 us (1%)
    all_to_all x1, waiting for transfers between devices, on_device(): lax.all_to_all(part_out, 'blk', split_axis=1, concat_axis=1, tiled=True)  357 us
    all_gather x1, waiting for transfers between devices, on_device(): gathered = lax.all_gather(queries, 'blk', axis=0, tiled=True)  150 us
    dynamic_slice x32, local copies, waits for them, and re-layouts, on_device(): partials, log_slots = lax.map(one_slot, (slot_queries, begins, local_block))  20.5 us
    all_to_all x1, waiting for transfers between devices, on_device(): lax.all_to_all(peak_out, 'blk', split_axis=1, concat_axis=1, tiled=True)  18.1 us
  transfers between devices with their start and end apart: 3, of which 3 were waited for; matrix products, arithmetic and copies ran while one was open for 4% of the time, Pallas kernels for 0%

commit v1 on v0

--- a/solution.py
+++ b/solution.py
@@ -64,7 +64,9 @@
     my_live = live_all[owner_dev]
     begins = tile_start[my_tiles]
     local_block = jnp.arange(slot_count, dtype=jnp.int32) // CAP
-    gathered = lax.all_gather(queries, "blk", axis=0, tiled=True)
+    gathered = jnp.concatenate(
+        lax.all_to_all(jnp.stack([queries] * lax.axis_size("blk")), "blk", 0, 0), axis=0
+    )
     slot_queries = jnp.transpose(jnp.take(gathered, my_tiles, axis=1), (1, 0, 2))
 
     def one_slot(inputs):

time: 730 us -> 1350 us (1.85)
  waiting for transfers between devices: 526 us -> 1110 us
  starting transfers between devices: 21.8 us -> 48.3 us
  local copies, waits for them, and re-layouts: 94.1 us -> 110 us
    all_to_all x0 -> x1, waiting for transfers between devices: none -> 737 us  [on_device(): lax.all_to_all(jnp.stack([queries] * lax.axis_size('blk')), 'blk', 0, 0)]
    all_gather x1 -> x0, waiting for transfers between devices: 150 us -> none  [on_device(): gathered = lax.all_gather(queries, 'blk', axis=0, tiled=True)]
    all_to_all x0 -> x1, starting transfers between devices: none -> 34.4 us  [on_device(): lax.all_to_all(jnp.stack([queries] * lax.axis_size('blk')), 'blk', 0, 0)]
  transfers between devices with their start and end apart: 3 -> 3, of which waited for: 3 -> 3; matrix products, arithmetic and copies ran while one was open for 4% -> 2% of each run, Pallas kernels for 0% -> 0%
where the time goes in v1:
time: 1350 us; the launch traced here: 1340 us
  waiting for transfers between devices  1110 us (82%)
  local copies, waits for them, and re-layouts  110 us (8%)
  starting transfers between devices  48.3 us (4%)
  other arithmetic  34.5 us (3%)
  matrix products  28.4 us (2%)
    all_to_all x1, waiting for transfers between devices, on_device(): lax.all_to_all(jnp.stack([queries] * lax.axis_size('blk')), 'blk', 0, 0)  737 us
    all_to_all x1, waiting for transfers between devices, on_device(): lax.all_to_all(part_out, 'blk', split_axis=1, concat_axis=1, tiled=True)  357 us
    all_to_all x1, starting transfers between devices, on_device(): lax.all_to_all(jnp.stack([queries] * lax.axis_size('blk')), 'blk', 0, 0)  34.4 us
  transfers between devices with their start and end apart: 3, of which 3 were waited for; matrix products, arithmetic and copies ran while one was open for 2% of the time, Pallas kernels for 0%

profile of v1, /device:TPU:38, one launch (start us, length us, event | category | flops | bytes accessed | tf_op | source)
XLA Modules:
  0.0 1344.3 jit_solution(7931290062621199775)
XLA Ops:
  1.1 5.6 stack.2
  6.7 34.4 %all-to-all-start = ((bf16[64,2,16,2048]{3,1,2,0:T(2,128)(2,1)}), bf16[64,2,16,2048]{3,1,2,0:T(2,128)(2,1)}, u32[]{:S(2)}, u32[]{:S(2)}) async-start(bf16[64,2,16,2048]{3,1,2,0:T(2,128)(2,1)} %stack.2), calls=%async_computation | async-start | bytes 16777216 | tf_op jit(solution)/shard_map/all_to_all | solution.py:68
  42.7 736.8 %all-to-all-done = bf16[64,2,16,2048]{3,1,2,0:T(2,128)(2,1)} async-done(((bf16[64,2,16,2048]{3,1,2,0:T(2,128)(2,1)}), bf16[64,2,16,2048]{3,1,2,0:T(2,128)(2,1)}, u32[]{:S(2)}, u32[]{:S(2)}) %all-to-all-start) | async-done | bytes 8388640 | tf_op jit(solution)/shard_map/all_to_all | solution.py:68
  779.5 8.0 copy.81
  787.4 13.1 reshape.201
  800.5 6.2 gather_fusion.1
  806.7 4.6 broadcast_select_fusion
  811.3 82.7 %while.14 = (s32[]{:T(128)}, bf16[8,128,2048]{1,2,0:T(8,128)(2,1)}, f32[8,128,16]{1,2,0:T(8,128)S(1)}, s32[8]{0:T(128)S(1)}, bf16[2048,512]{1,0:T(8,128)(2,1)}, ...) while((s32[]{:T(128)}, bf16[8,128,2048]{1,2,0:T(8,128)(2,1)}, ...), condition=%wide.region_7.8_spmd, body=%wide.region_4.7_spmd.sunk | while | flops 550828672 | bytes 22361340 | solution.py:80
  812.6 1.3 constant_dynamic-slice_fusion.6
  874.6 1.3 constant_dynamic-slice_fusion.6
  884.9 1.3 constant_dynamic-slice_fusion.6
  895.2 6.5 all-to-all-start.1
  901.7 6.7 copy.91
  908.4 18.1 %all-to-all-done.1 = f32[64,1,256]{2,1,0:T(1,128)S(1)} async-done(((f32[64,1,256]{2,1,0:T(1,128)}), f32[64,1,256]{2,1,0:T(1,128)S(1)}, u32[]{:S(2)}, u32[]{:S(2)}) %all-to-all-start.1) | async-done | bytes 65568 | tf_op jit(solution)/shard_map/all_to_all | solution.py:85
  926.5 7.5 all-to-all-start.2
  936.6 2.1 gather_fusion.2
  938.7 1.8 exponential_select_fusion
  941.1 5.1 mul.35
  946.3 9.3 mul.36
  955.5 357.2 %all-to-all-done.2 = bf16[8,64,2,2048]{3,0,2,1:T(8,128)(2,1)} async-done(((bf16[8,64,2,2048]{3,0,2,1:T(8,128)(2,1)}), bf16[8,64,2,2048]{3,0,2,1:T(8,128)(2,1)}, u32[]{:S(2)}, u32[]{:S(2)}) %all-to-all-start.2) | async-done | bytes 4194336 | tf_op jit(solution)/shard_map/all_to_all | solution.py:84
  1312.8 7.8 copy.92
  1320.6 11.7 bitcast_multiply_fusion
  1332.3 6.1 fusion.13
  1338.7 5.6 convolution_convert_fusion
  (173 shorter events, 75.8 us)
Async XLA Ops:
  0.0 42.0 %copy-start = (s32[16]{0:T(128)S(1)}, s32[16]{0:T(128)}, u32[]{:S(2)}) copy-start(s32[16]{0:T(128)} %param.13) | copy-start | bytes 196
  6.7 34.4 %copy-start.2 = (s32[16,12]{1,0:T(8,128)S(1)}, s32[16,12]{1,0:T(8,128)}, u32[]{:S(2)}) copy-start(s32[16,12]{1,0:T(8,128)} %param.12) | copy-start | bytes 2308
  6.7 772.8 %all-to-all-start = ((bf16[64,2,16,2048]{3,1,2,0:T(2,128)(2,1)}), bf16[64,2,16,2048]{3,1,2,0:T(2,128)(2,1)}, u32[]{:S(2)}, u32[]{:S(2)}) async-start(bf16[64,2,16,2048]{3,1,2,0:T(2,128)(2,1)} %stack.2), calls=%async_computation | async-start | bytes 16777216 | tf_op jit(solution)/shard_map/all_to_all | solution.py:68
  895.2 31.3 %all-to-all-start.1 = ((f32[64,1,256]{2,1,0:T(1,128)}), f32[64,1,256]{2,1,0:T(1,128)S(1)}, u32[]{:S(2)}, u32[]{:S(2)}) async-start(f32[64,1,256]{2,1,0:T(1,128)} %reshape.236), calls=%async_computation.1 | async-start | bytes 131072 | tf_op jit(solution)/shard_map/all_to_all | solution.py:85
  926.5 386.3 %all-to-all-start.2 = ((bf16[8,64,2,2048]{3,0,2,1:T(8,128)(2,1)}), bf16[8,64,2,2048]{3,0,2,1:T(8,128)(2,1)}, u32[]{:S(2)}, u32[]{:S(2)}) async-start(bf16[8,64,2,2048]{3,0,2,1:T(8,128)(2,1)} %bitcast.116), calls=%async_computation.2 | async-start | bytes 8388608 | tf_op jit(solution)/shard_map/all_to_all | solution.py:84
  1338.5 5.7 copy-start.1
